TPU v7x, 32 devices: a whole 2x2x4 slice. The times are simulated.
32 devices in a mesh: region: 8 (over z, y), blk: 4 (over x, core).
Axes of the slice: x: 2, y: 2, z: 4, core: 2. Of those that a mesh axis runs over, the one named last changes fastest.
Arguments:
- jac_bus: float32 [256, 8, 128, 128], P('region', 'blk'), may hold values from -0.1875 to 0.1875
- pattern: int32 [256, 8], P(('region', 'blk')), may hold values from 0 to 23
- branch_weight: float32 [256, 128], P(('region', 'blk')), may hold values from 0.2 to 5
- bus_diag: float32 [256, 128], P(('region', 'blk')), may hold values from 0.3 to 3
- right_side: float32 [256, 128], P(('region', 'blk')), may hold values from -8 to 8
Outputs:
- solution: float32 [256, 128], P(('region', 'blk'))
- residual: float32 [256, 128], P(('region', 'blk'))
Inputs may be any that keep to these rules, and one draw needn't show every extreme that they name: pattern values below 8 name the region before the branch tile's region, those from 16 the region after it, with regions closed into a loop.
All inputs are finite; a program needn't handle non-finite values.
Results may differ from a plain program's by a relative error of at most 0.0003.
Values sent between devices are 32-bit elements; how exact they have to be, the bound alone decides.
No kernel may reach another device: no remote copies, remote signals or barrier semaphores. Data moves between devices by JAX's collectives and lax.ppermute only.
A program may use at most 64 MiB of HBM per device.

v0:
```python
import jax
import jax.numpy as jnp
from jax import lax
from jax.sharding import PartitionSpec as P

ITERS = 12


def extended(array, sides, width):
    for axis, dim in sides:
        size, length = (lax.axis_size(axis), array.shape[dim])
        up = [(i, (i + 1) % size) for i in range(size)]
        down = [(j, i) for i, j in up]
        last = lax.slice_in_dim(array, length - width, length, axis=dim)
        leading = lax.slice_in_dim(array, 0, width, axis=dim)
        before = lax.ppermute(last, axis, up)
        after = lax.ppermute(leading, axis, down)
        array = jnp.concatenate([before, array, after], axis=dim)
    return array


def from_behind(array, axis, by):
    length = lax.axis_size(axis)
    return lax.ppermute(array, axis, [(i, (i + by) % length) for i in range(length)])


def neighbours(values):
    return extended(values[None], (("region", 0),), 1)


def route(lower, middle, upper):
    from_upper = from_behind(lower, "region", -1)
    from_lower = from_behind(upper, "region", 1)
    return middle + from_upper + from_lower


def spread(tiles, weight, index, count):
    back = jnp.einsum("tjab,ta->tjb", tiles, weight, precision=lax.Precision.HIGHEST)
    width = back.shape[-1]
    return jnp.zeros((count, width), jnp.float32).at[index.reshape(-1)].add(back.reshape(-1, width))


def body(jac_bus, pattern, branch_weight, bus_diag, right_side):
    hp = lax.Precision.HIGHEST
    blocks = lax.axis_size("blk")
    per_dev = right_side.shape[0]
    width = right_side.shape[1]
    group_len = jac_bus.shape[1]
    tiles = lax.all_to_all(jac_bus, "blk", split_axis=0, concat_axis=1, tiled=True)
    group = jnp.arange(tiles.shape[1], dtype=jnp.int32) // group_len
    index = pattern // per_dev * (blocks * per_dev) + group[None, :] * per_dev + pattern % per_dev

    def collect(buffer):
        parts = buffer.reshape(3, blocks, per_dev, width)
        total = route(parts[0], parts[1], parts[2])
        return lax.psum_scatter(total, "blk", scatter_dimension=0, tiled=True)[0]

    def branch_rows(vector):
        region_vals = lax.all_gather(vector[None], "blk", axis=0, tiled=True)
        flat = neighbours(region_vals).reshape(-1, width)
        return jnp.einsum("tjab,tjb->ta", tiles, flat[index], precision=hp)

    count = 3 * blocks * per_dev

    def apply_operator(vector):
        rows = branch_rows(vector)
        return bus_diag * vector + collect(spread(tiles, branch_weight * rows, index, count))

    precond = bus_diag + collect(spread(tiles * tiles, branch_weight, index, count))
    solution = jnp.zeros_like(right_side)
    residual = right_side

    def paired(resid):
        scaled = resid / precond
        image = apply_operator(scaled)
        gamma, delta = lax.psum(
            (jnp.sum(resid * scaled), jnp.sum(image * scaled)), ("region", "blk")
        )
        return (scaled, image, gamma, delta)

    scaled, image, gamma, delta = paired(residual)
    alpha = gamma / delta
    direction, along = (scaled, image)
    solution = alpha * direction
    residual = residual - alpha * along

    def one_step(step, carry):
        solution, residual, direction, along, gamma, alpha = carry
        scaled, image, fresh, delta = paired(residual)
        beta = fresh / gamma
        alpha = fresh / (delta - beta * fresh / alpha)
        direction = scaled + beta * direction
        along = image + beta * along
        solution = solution + alpha * direction
        residual = residual - alpha * along
        return (solution, residual, direction, along, fresh, alpha)

    carry = lax.fori_loop(
        0, ITERS - 1, one_step, (solution, residual, direction, along, gamma, alpha)
    )
    solution, residual = (carry[0], carry[1])
    return (solution, residual)


def solution(mesh):
    return jax.shard_map(
        body,
        mesh=mesh,
        in_specs=(
            P("region", "blk", None, None),
            P(("region", "blk"), None),
            P(("region", "blk"), None),
            P(("region", "blk"), None),
            P(("region", "blk"), None),
        ),
        out_specs=(P(("region", "blk"), None), P(("region", "blk"), None)),
        check_vma=False,
    )
```

profile of v0, /device:TPU:14, one launch (start us, length us, event | category | flops | bytes accessed | tf_op | source)
XLA Modules:
  0.0 1099.4 jit_solution(10616008818148607382)
XLA Ops:
  0.6 5.4 all-to-all-start
  6.1 46.5 %all-to-all-done = f32[32,2,128,128]{3,2,1,0:T(8,128)} async-done(((f32[32,2,128,128]{3,2,1,0:T(8,128)}), f32[32,2,128,128]{3,2,1,0:T(8,128)}, u32[]{:S(2)}, u32[]{:S(2)}) %all-to-all-start) | async-done | bytes 4194336 | tf_op jit(solution)/shard_map/all_to_all | solution.py:49
  64.9 10.1 all-reduce.1
  75.7 5.2 all-gather.1
  85.3 3.2 collective-permute-done.7
  89.1 5.4 fusion.33
  102.3 10.1 all-reduce.2
  113.6 51.1 %all-reduce.4 = (f32[]{:T(128)}, f32[]{:T(128)}) all-reduce(f32[]{:T(128)} %get-tuple-element.70, f32[]{:T(128)} %get-tuple-element.69), channel_id=1, replica_groups=mesh['region'=8,'blk'=4] {'region','blk'}, use_global_device_ids=true, to_apply=%region_3.4 | all-reduce | flops 2 | bytes 16 | tf_op jit(solution)/shard_map/psum | solution.py:76
  166.0 932.8 %while.21 = (s32[]{:T(128)}, f32[8,128]{1,0:T(8,128)S(1)}, f32[8,128]{1,0:T(8,128)S(1)}, f32[8,128]{1,0:T(8,128)S(1)}, f32[8,128]{1,0:T(8,128)S(1)}, /*index=5*/...) while((s32[]{:T(128)}, f32[8,128]{1,0:T(8,128)S(1)}, ...), condition=%wide.wide.region_15.16_spmd, body=%wide.wide.region_8.15_spmd.sunk | while | flops 25230720 | bytes 25991660 | solution.py:98
  166.0 5.2 all-gather.4
  177.0 5.4 fusion.68
  189.2 3.2 collective-permute-done.3
  192.4 10.1 all-reduce.9
  203.8 44.6 %all-reduce.10 = (f32[]{:T(128)}, f32[]{:T(128)}) all-reduce(f32[]{:T(128)} %get-tuple-element.267, f32[]{:T(128)} %get-tuple-element.268), channel_id=1, replica_groups=mesh['region'=8,'blk'=4] {'region','blk'}, use_global_device_ids=true, to_apply=%region_10.10 | all-reduce | flops 2 | bytes 16 | tf_op jit(solution)/shard_map/while/body/eval_jaxpr/psum | solution.py:76
  251.4 5.2 all-gather.4
  261.8 5.4 fusion.68
  274.6 3.2 collective-permute-done.3
  277.8 10.1 all-reduce.9
  289.2 43.4 %all-reduce.10 = (f32[]{:T(128)}, f32[]{:T(128)}) all-reduce(f32[]{:T(128)} %get-tuple-element.267, f32[]{:T(128)} %get-tuple-element.268), channel_id=1, replica_groups=mesh['region'=8,'blk'=4] {'region','blk'}, use_global_device_ids=true, to_apply=%region_10.10 | all-reduce | flops 2 | bytes 16 | tf_op jit(solution)/shard_map/while/body/eval_jaxpr/psum | solution.py:76
  335.5 5.2 all-gather.4
  346.5 5.4 fusion.68
  358.7 3.2 collective-permute-done.3
  361.9 10.1 all-reduce.9
  373.3 44.6 %all-reduce.10 = (f32[]{:T(128)}, f32[]{:T(128)}) all-reduce(f32[]{:T(128)} %get-tuple-element.267, f32[]{:T(128)} %get-tuple-element.268), channel_id=1, replica_groups=mesh['region'=8,'blk'=4] {'region','blk'}, use_global_device_ids=true, to_apply=%region_10.10 | all-reduce | flops 2 | bytes 16 | tf_op jit(solution)/shard_map/while/body/eval_jaxpr/psum | solution.py:76
  420.9 5.2 all-gather.4
  431.3 5.4 fusion.68
  444.1 3.2 collective-permute-done.3
  447.3 10.1 all-reduce.9
  458.7 43.4 %all-reduce.10 = (f32[]{:T(128)}, f32[]{:T(128)}) all-reduce(f32[]{:T(128)} %get-tuple-element.267, f32[]{:T(128)} %get-tuple-element.268), channel_id=1, replica_groups=mesh['region'=8,'blk'=4] {'region','blk'}, use_global_device_ids=true, to_apply=%region_10.10 | all-reduce | flops 2 | bytes 16 | tf_op jit(solution)/shard_map/while/body/eval_jaxpr/psum | solution.py:76
  505.0 5.2 all-gather.4
  516.0 5.4 fusion.68
  528.2 3.2 collective-permute-done.3
  531.4 10.1 all-reduce.9
  542.8 44.6 %all-reduce.10 = (f32[]{:T(128)}, f32[]{:T(128)}) all-reduce(f32[]{:T(128)} %get-tuple-element.267, f32[]{:T(128)} %get-tuple-element.268), channel_id=1, replica_groups=mesh['region'=8,'blk'=4] {'region','blk'}, use_global_device_ids=true, to_apply=%region_10.10 | all-reduce | flops 2 | bytes 16 | tf_op jit(solution)/shard_map/while/body/eval_jaxpr/psum | solution.py:76
  590.3 5.2 all-gather.4
  600.8 5.4 fusion.68
  613.5 3.2 collective-permute-done.3
  616.7 10.1 all-reduce.9
  628.1 43.4 %all-reduce.10 = (f32[]{:T(128)}, f32[]{:T(128)}) all-reduce(f32[]{:T(128)} %get-tuple-element.267, f32[]{:T(128)} %get-tuple-element.268), channel_id=1, replica_groups=mesh['region'=8,'blk'=4] {'region','blk'}, use_global_device_ids=true, to_apply=%region_10.10 | all-reduce | flops 2 | bytes 16 | tf_op jit(solution)/shard_map/while/body/eval_jaxpr/psum | solution.py:76
  674.5 5.2 all-gather.4
  685.4 5.4 fusion.68
  697.7 3.2 collective-permute-done.3
  700.9 10.1 all-reduce.9
  712.3 44.6 %all-reduce.10 = (f32[]{:T(128)}, f32[]{:T(128)}) all-reduce(f32[]{:T(128)} %get-tuple-element.267, f32[]{:T(128)} %get-tuple-element.268), channel_id=1, replica_groups=mesh['region'=8,'blk'=4] {'region','blk'}, use_global_device_ids=true, to_apply=%region_10.10 | all-reduce | flops 2 | bytes 16 | tf_op jit(solution)/shard_map/while/body/eval_jaxpr/psum | solution.py:76
  759.8 5.2 all-gather.4
  770.3 5.4 fusion.68
  783.0 3.2 collective-permute-done.3
  786.2 10.1 all-reduce.9
  797.6 43.4 %all-reduce.10 = (f32[]{:T(128)}, f32[]{:T(128)}) all-reduce(f32[]{:T(128)} %get-tuple-element.267, f32[]{:T(128)} %get-tuple-element.268), channel_id=1, replica_groups=mesh['region'=8,'blk'=4] {'region','blk'}, use_global_device_ids=true, to_apply=%region_10.10 | all-reduce | flops 2 | bytes 16 | tf_op jit(solution)/shard_map/while/body/eval_jaxpr/psum | solution.py:76
  844.0 5.2 all-gather.4
  854.9 5.4 fusion.68
  867.2 3.2 collective-permute-done.3
  870.4 10.1 all-reduce.9
  881.8 44.6 %all-reduce.10 = (f32[]{:T(128)}, f32[]{:T(128)}) all-reduce(f32[]{:T(128)} %get-tuple-element.267, f32[]{:T(128)} %get-tuple-element.268), channel_id=1, replica_groups=mesh['region'=8,'blk'=4] {'region','blk'}, use_global_device_ids=true, to_apply=%region_10.10 | all-reduce | flops 2 | bytes 16 | tf_op jit(solution)/shard_map/while/body/eval_jaxpr/psum | solution.py:76
  929.3 5.2 all-gather.4
  939.8 5.4 fusion.68
  952.5 3.2 collective-permute-done.3
  955.7 10.1 all-reduce.9
  967.1 43.4 %all-reduce.10 = (f32[]{:T(128)}, f32[]{:T(128)}) all-reduce(f32[]{:T(128)} %get-tuple-element.267, f32[]{:T(128)} %get-tuple-element.268), channel_id=1, replica_groups=mesh['region'=8,'blk'=4] {'region','blk'}, use_global_device_ids=true, to_apply=%region_10.10 | all-reduce | flops 2 | bytes 16 | tf_op jit(solution)/shard_map/while/body/eval_jaxpr/psum | solution.py:76
  1013.4 5.2 all-gather.4
  1024.4 5.4 fusion.68
  1036.6 3.2 collective-permute-done.3
  1039.8 10.1 all-reduce.9
  1051.3 44.6 %all-reduce.10 = (f32[]{:T(128)}, f32[]{:T(128)}) all-reduce(f32[]{:T(128)} %get-tuple-element.267, f32[]{:T(128)} %get-tuple-element.268), channel_id=1, replica_groups=mesh['region'=8,'blk'=4] {'region','blk'}, use_global_device_ids=true, to_apply=%region_10.10 | all-reduce | flops 2 | bytes 16 | tf_op jit(solution)/shard_map/while/body/eval_jaxpr/psum | solution.py:76
  (316 shorter events, 180.7 us)
Async XLA Ops:
  0.6 52.0 %all-to-all-start = ((f32[32,2,128,128]{3,2,1,0:T(8,128)}), f32[32,2,128,128]{3,2,1,0:T(8,128)}, u32[]{:S(2)}, u32[]{:S(2)}) async-start(f32[32,2,128,128]{3,2,1,0:T(8,128)} %param.7), calls=%async_computation | async-start | bytes 8388608 | tf_op jit(solution)/shard_map/all_to_all | solution.py:49
  55.1 8.2 copy-start.9
  55.1 19.9 %copy-start.4 = (f32[8,128]{1,0:T(8,128)S(1)}, f32[8,128]{1,0:T(8,128)}, u32[]{:S(2)}) copy-start(f32[8,128]{1,0:T(8,128)} %param.10) | copy-start | bytes 12292
  55.1 19.9 %copy-start.7 = (f32[8,128]{1,0:T(8,128)S(1)}, f32[8,128]{1,0:T(8,128)}, u32[]{:S(2)}) copy-start(f32[8,128]{1,0:T(8,128)} %param.11) | copy-start | bytes 12292
  60.2 4.7 collective-permute-start.4
  60.8 4.1 collective-permute-start.5
  80.9 4.4 collective-permute-start.6
  83.8 4.6 collective-permute-start.7
  89.1 5.4 copy-start.1
  97.4 4.7 collective-permute-start.8
  97.5 4.8 collective-permute-start.9
  171.2 4.6 collective-permute-start
  172.6 3.7 collective-permute-start.1
  177.0 5.4 copy-start.2
  185.3 3.9 collective-permute-start.2
  187.8 4.6 collective-permute-start.3
  256.6 4.6 collective-permute-start
  256.8 4.4 collective-permute-start.1
  261.8 5.4 copy-start.2
  270.2 4.4 collective-permute-start.2
  273.1 4.6 collective-permute-start.3
  340.7 4.6 collective-permute-start
  342.1 3.7 collective-permute-start.1
  346.5 5.4 copy-start.2
  354.8 3.9 collective-permute-start.2
  357.3 4.6 collective-permute-start.3
  426.1 4.6 collective-permute-start
  426.3 4.4 collective-permute-start.1
  431.3 5.4 copy-start.2
  439.6 4.4 collective-permute-start.2
  442.6 4.6 collective-permute-start.3
  510.2 4.6 collective-permute-start
  511.6 3.7 collective-permute-start.1
  516.0 5.4 copy-start.2
  524.3 3.9 collective-permute-start.2
  526.8 4.6 collective-permute-start.3
  595.5 4.6 collective-permute-start
  595.8 4.4 collective-permute-start.1
  600.8 5.4 copy-start.2
  609.1 4.4 collective-permute-start.2
  612.1 4.6 collective-permute-start.3
  679.7 4.6 collective-permute-start
  681.1 3.7 collective-permute-start.1
  685.4 5.4 copy-start.2
  693.8 3.9 collective-permute-start.2
  696.2 4.6 collective-permute-start.3
  765.0 4.6 collective-permute-start
  765.2 4.4 collective-permute-start.1
  770.3 5.4 copy-start.2
  778.6 4.4 collective-permute-start.2
  781.6 4.6 collective-permute-start.3
  849.2 4.6 collective-permute-start
  850.6 3.7 collective-permute-start.1
  854.9 5.4 copy-start.2
  863.3 3.9 collective-permute-start.2
  865.7 4.6 collective-permute-start.3
  934.5 4.6 collective-permute-start
  934.7 4.4 collective-permute-start.1
  948.1 4.4 collective-permute-start.2
  951.1 4.6 collective-permute-start.3
  1018.7 4.6 collective-permute-start
  1020.1 3.7 collective-permute-start.1
  1032.7 3.9 collective-permute-start.2
  1035.2 4.6 collective-permute-start.3
  (7 other events, 23.7 us)
where the time goes:
time: 1100 us
  blocking collectives  729 us (66%)
  waiting for transfers between devices  113 us (10%)
  matrix products  92.2 us (8%)
  starting transfers between devices  76.1 us (7%)
  other arithmetic  34 us (3%)
  loops' own time  32.3 us (3%)
  local copies, waits for them, and re-layouts  20.5 us (2%)
    psum x12, blocking collectives, paired(): lax.psum((jnp.sum(resid * scaled), jnp.sum(image * scaled)), ('region', '...  535 us
    while x11, blocking collectives  111 us
    dot_general x12, matrix products, branch_rows(): return jnp.einsum('tjab,tjb->ta', tiles, flat[index], precision=hp)  64.8 us
    all_gather x12, blocking collectives, branch_rows(): region_vals = lax.all_gather(vector[None], 'blk', axis=0, tiled=True)  62.5 us
    all_to_all x1, waiting for transfers between devices, body(): lax.all_to_all(jac_bus, 'blk', split_axis=0, concat_axis=1, tiled=True)  46.5 us
    ppermute x26, waiting for transfers between devices, from_behind(): lax.ppermute(array, axis, [(i, (i + by) % length) for i in range(length)])  41.1 us
    ppermute x26, starting transfers between devices, from_behind(): lax.ppermute(array, axis, [(i, (i + by) % length) for i in range(length)])  35.6 us
    another operation x1, loops' own time, body(): lax.fori_loop(0, ITERS - 1, one_step, (solution, residual, direction, alo...  32.3 us
  transfers between devices with their start and end apart: 51, of which 45 were waited for; matrix products, arithmetic and copies ran while one was open for 1% of the time, Pallas kernels for 0%

commit v1 on v0

--- a/solution.py
+++ b/solution.py
@@ -74,7 +74,7 @@
         scaled = resid / precond
         image = apply_operator(scaled)
         gamma, delta = lax.psum(
-            (jnp.sum(resid * scaled), jnp.sum(image * scaled)), ("region", "blk")
+            lax.psum((jnp.sum(resid * scaled), jnp.sum(image * scaled)), "blk"), "region"
         )
         return (scaled, image, gamma, delta)
 

time: 1100 us -> 931 us (0.85); the launches traced: 1100 us -> 919 us
  blocking collectives: 729 us -> 532 us
  starting transfers between devices: 76.1 us -> 95.6 us
    psum x12 -> x24, blocking collectives: 535 us -> 337 us  [the longest x12 261 us: paired(): lax.psum(lax.psum((jnp.sum(resid * scaled), jnp.sum(image * scaled)), 'bl...]
    ppermute x12, starting transfers between devices: 9.62 us -> 47.2 us  [extended(): after = lax.ppermute(leading, axis, down)]
    ppermute x12, waiting for transfers between devices: 4.52 us -> 26.2 us  [extended(): before = lax.ppermute(last, axis, up)]
    ppermute x26, waiting for transfers between devices: 41.1 us -> 20.6 us  [from_behind(): lax.ppermute(array, axis, [(i, (i + by) % length) for i in range(length)])]
    ppermute x12, starting transfers between devices: 25.5 us -> 5.83 us  [extended(): before = lax.ppermute(last, axis, up)]
  transfers between devices with their start and end apart: 51 -> 51, of which waited for: 45 -> 50; matrix products, arithmetic and copies ran while one was open for 1% -> 1% of each run, Pallas kernels for 0% -> 0%
where the time goes in v1:
time: 931 us; the launch traced here: 919 us
  blocking collectives  532 us (57%)
  waiting for transfers between devices  111 us (12%)
  starting transfers between devices  95.6 us (10%)
  matrix products  92.2 us (10%)
  other arithmetic  33.1 us (4%)
  loops' own time  32.3 us (3%)
  local copies, waits for them, and re-layouts  20.5 us (2%)
    psum x12, blocking collectives, paired(): lax.psum(lax.psum((jnp.sum(resid * scaled), jnp.sum(image * scaled)), 'bl...  261 us
    while x11, blocking collectives  111 us
    psum x12, blocking collectives, paired(): lax.psum((jnp.sum(resid * scaled), jnp.sum(image * scaled)), 'blk')  76.2 us
    dot_general x12, matrix products, branch_rows(): return jnp.einsum('tjab,tjb->ta', tiles, flat[index], precision=hp)  64.8 us
    all_gather x12, blocking collectives, branch_rows(): region_vals = lax.all_gather(vector[None], 'blk', axis=0, tiled=True)  63.1 us
    ppermute x12, starting transfers between devices, extended(): after = lax.ppermute(leading, axis, down)  47.2 us
    all_to_all x1, waiting for transfers between devices, body(): lax.all_to_all(jac_bus, 'blk', split_axis=0, concat_axis=1, tiled=True)  46.5 us
    ppermute x26, starting transfers between devices, from_behind(): lax.ppermute(array, axis, [(i, (i + by) % length) for i in range(length)])  37.2 us
  transfers between devices with their start and end apart: 51, of which 50 were waited for; matrix products, arithmetic and copies ran while one was open for 1% of the time, Pallas kernels for 0%

profile of v1, /device:TPU:14, one launch (start us, length us, event | category | flops | bytes accessed | tf_op | source)
XLA Modules:
  0.0 918.8 jit_solution(10062033673107678733)
XLA Ops:
  0.6 5.4 all-to-all-start
  6.1 46.5 %all-to-all-done = f32[32,2,128,128]{3,2,1,0:T(8,128)} async-done(((f32[32,2,128,128]{3,2,1,0:T(8,128)}), f32[32,2,128,128]{3,2,1,0:T(8,128)}, u32[]{:S(2)}, u32[]{:S(2)}) %all-to-all-start) | async-done | bytes 4194336 | tf_op jit(solution)/shard_map/all_to_all | solution.py:49
  64.9 10.1 %all-reduce.1 = f32[4,8,128]{2,1,0:T(8,128)S(1)} all-reduce(f32[4,8,128]{2,1,0:T(8,128)S(1)} %fusion.15), channel_id=5, replica_groups=mesh['region'=8,'blk'=4] {'blk'}, use_global_device_ids=true, to_apply=%region_1.2.clone | all-reduce | flops 4096 | bytes 32768
  75.7 5.2 all-gather.1
  89.1 5.4 fusion.33
  102.3 10.1 %all-reduce.2 = f32[4,8,128]{2,1,0:T(8,128)S(1)} all-reduce(f32[4,8,128]{2,1,0:T(8,128)S(1)} %fusion.13), channel_id=6, replica_groups=mesh['region'=8,'blk'=4] {'blk'}, use_global_device_ids=true, to_apply=%region_6.7.clone | all-reduce | flops 4096 | bytes 32768
  113.7 6.3 all-reduce.6
  119.9 27.2 %all-reduce.5 = (f32[]{:T(128)}, f32[]{:T(128)}) all-reduce(f32[]{:T(128)} %get-tuple-element.101, f32[]{:T(128)} %get-tuple-element.102), channel_id=1, replica_groups=mesh['region'=8,'blk'=4] {'region'}, use_global_device_ids=true, to_apply=%region_4.5 | all-reduce | flops 2 | bytes 16 | tf_op jit(solution)/shard_map/psum | solution.py:76
  148.4 769.8 %while.21 = (s32[]{:T(128)}, f32[8,128]{1,0:T(8,128)S(1)}, f32[8,128]{1,0:T(8,128)S(1)}, f32[8,128]{1,0:T(8,128)S(1)}, f32[8,128]{1,0:T(8,128)S(1)}, /*index=5*/...) while((s32[]{:T(128)}, f32[8,128]{1,0:T(8,128)S(1)}, ...), condition=%wide.wide.region_19.20_spmd, body=%wide.wide.region_10.19_spmd.sunk | while | flops 25230724 | bytes 25991676 | solution.py:98
  148.4 5.2 all-gather.4
  160.7 5.4 fusion.68
  174.8 10.1 %all-reduce.13 = f32[4,8,128]{2,1,0:T(8,128)S(1)} all-reduce(f32[4,8,128]{2,1,0:T(8,128)S(1)} %fusion.70), channel_id=4, replica_groups=mesh['region'=8,'blk'=4] {'blk'}, use_global_device_ids=true, to_apply=%region_15.15.clone | all-reduce | flops 4096 | bytes 32768 | tf_op jit(solution)/shard_map/while
  186.1 6.4 all-reduce.14
  192.5 20.4 %all-reduce.15 = (f32[]{:T(128)}, f32[]{:T(128)}) all-reduce(f32[]{:T(128)} %get-tuple-element.277, f32[]{:T(128)} %get-tuple-element.278), channel_id=1, replica_groups=mesh['region'=8,'blk'=4] {'region'}, use_global_device_ids=true, to_apply=%region_13.13 | all-reduce | flops 2 | bytes 16 | tf_op jit(solution)/shard_map/while/body/eval_jaxpr/psum | solution.py:76
  215.9 5.2 all-gather.4
  230.2 5.4 fusion.68
  244.1 10.1 %all-reduce.13 = f32[4,8,128]{2,1,0:T(8,128)S(1)} all-reduce(f32[4,8,128]{2,1,0:T(8,128)S(1)} %fusion.70), channel_id=4, replica_groups=mesh['region'=8,'blk'=4] {'blk'}, use_global_device_ids=true, to_apply=%region_15.15.clone | all-reduce | flops 4096 | bytes 32768 | tf_op jit(solution)/shard_map/while
  255.4 6.4 all-reduce.14
  261.8 21.3 %all-reduce.15 = (f32[]{:T(128)}, f32[]{:T(128)}) all-reduce(f32[]{:T(128)} %get-tuple-element.277, f32[]{:T(128)} %get-tuple-element.278), channel_id=1, replica_groups=mesh['region'=8,'blk'=4] {'region'}, use_global_device_ids=true, to_apply=%region_13.13 | all-reduce | flops 2 | bytes 16 | tf_op jit(solution)/shard_map/while/body/eval_jaxpr/psum | solution.py:76
  286.1 5.2 all-gather.4
  300.4 5.4 fusion.68
  314.3 10.1 %all-reduce.13 = f32[4,8,128]{2,1,0:T(8,128)S(1)} all-reduce(f32[4,8,128]{2,1,0:T(8,128)S(1)} %fusion.70), channel_id=4, replica_groups=mesh['region'=8,'blk'=4] {'blk'}, use_global_device_ids=true, to_apply=%region_15.15.clone | all-reduce | flops 4096 | bytes 32768 | tf_op jit(solution)/shard_map/while
  325.6 6.4 all-reduce.14
  332.0 21.3 %all-reduce.15 = (f32[]{:T(128)}, f32[]{:T(128)}) all-reduce(f32[]{:T(128)} %get-tuple-element.277, f32[]{:T(128)} %get-tuple-element.278), channel_id=1, replica_groups=mesh['region'=8,'blk'=4] {'region'}, use_global_device_ids=true, to_apply=%region_13.13 | all-reduce | flops 2 | bytes 16 | tf_op jit(solution)/shard_map/while/body/eval_jaxpr/psum | solution.py:76
  356.2 5.2 all-gather.4
  370.5 5.4 fusion.68
  384.5 10.1 %all-reduce.13 = f32[4,8,128]{2,1,0:T(8,128)S(1)} all-reduce(f32[4,8,128]{2,1,0:T(8,128)S(1)} %fusion.70), channel_id=4, replica_groups=mesh['region'=8,'blk'=4] {'blk'}, use_global_device_ids=true, to_apply=%region_15.15.clone | all-reduce | flops 4096 | bytes 32768 | tf_op jit(solution)/shard_map/while
  395.8 6.4 all-reduce.14
  402.1 21.3 %all-reduce.15 = (f32[]{:T(128)}, f32[]{:T(128)}) all-reduce(f32[]{:T(128)} %get-tuple-element.277, f32[]{:T(128)} %get-tuple-element.278), channel_id=1, replica_groups=mesh['region'=8,'blk'=4] {'region'}, use_global_device_ids=true, to_apply=%region_13.13 | all-reduce | flops 2 | bytes 16 | tf_op jit(solution)/shard_map/while/body/eval_jaxpr/psum | solution.py:76
  426.4 5.3 all-gather.4
  440.8 5.4 fusion.68
  454.7 10.1 %all-reduce.13 = f32[4,8,128]{2,1,0:T(8,128)S(1)} all-reduce(f32[4,8,128]{2,1,0:T(8,128)S(1)} %fusion.70), channel_id=4, replica_groups=mesh['region'=8,'blk'=4] {'blk'}, use_global_device_ids=true, to_apply=%region_15.15.clone | all-reduce | flops 4096 | bytes 32768 | tf_op jit(solution)/shard_map/while
  466.0 6.4 all-reduce.14
  472.4 21.3 %all-reduce.15 = (f32[]{:T(128)}, f32[]{:T(128)}) all-reduce(f32[]{:T(128)} %get-tuple-element.277, f32[]{:T(128)} %get-tuple-element.278), channel_id=1, replica_groups=mesh['region'=8,'blk'=4] {'region'}, use_global_device_ids=true, to_apply=%region_13.13 | all-reduce | flops 2 | bytes 16 | tf_op jit(solution)/shard_map/while/body/eval_jaxpr/psum | solution.py:76
  496.7 5.3 all-gather.4
  511.0 5.4 fusion.68
  525.0 10.1 %all-reduce.13 = f32[4,8,128]{2,1,0:T(8,128)S(1)} all-reduce(f32[4,8,128]{2,1,0:T(8,128)S(1)} %fusion.70), channel_id=4, replica_groups=mesh['region'=8,'blk'=4] {'blk'}, use_global_device_ids=true, to_apply=%region_15.15.clone | all-reduce | flops 4096 | bytes 32768 | tf_op jit(solution)/shard_map/while
  536.3 6.4 all-reduce.14
  542.6 21.3 %all-reduce.15 = (f32[]{:T(128)}, f32[]{:T(128)}) all-reduce(f32[]{:T(128)} %get-tuple-element.277, f32[]{:T(128)} %get-tuple-element.278), channel_id=1, replica_groups=mesh['region'=8,'blk'=4] {'region'}, use_global_device_ids=true, to_apply=%region_13.13 | all-reduce | flops 2 | bytes 16 | tf_op jit(solution)/shard_map/while/body/eval_jaxpr/psum | solution.py:76
  566.9 5.3 all-gather.4
  581.3 5.4 fusion.68
  595.2 10.1 %all-reduce.13 = f32[4,8,128]{2,1,0:T(8,128)S(1)} all-reduce(f32[4,8,128]{2,1,0:T(8,128)S(1)} %fusion.70), channel_id=4, replica_groups=mesh['region'=8,'blk'=4] {'blk'}, use_global_device_ids=true, to_apply=%region_15.15.clone | all-reduce | flops 4096 | bytes 32768 | tf_op jit(solution)/shard_map/while
  606.5 6.4 all-reduce.14
  612.9 21.3 %all-reduce.15 = (f32[]{:T(128)}, f32[]{:T(128)}) all-reduce(f32[]{:T(128)} %get-tuple-element.277, f32[]{:T(128)} %get-tuple-element.278), channel_id=1, replica_groups=mesh['region'=8,'blk'=4] {'region'}, use_global_device_ids=true, to_apply=%region_13.13 | all-reduce | flops 2 | bytes 16 | tf_op jit(solution)/shard_map/while/body/eval_jaxpr/psum | solution.py:76
  637.2 5.3 all-gather.4
  651.5 5.4 fusion.68
  665.5 10.1 %all-reduce.13 = f32[4,8,128]{2,1,0:T(8,128)S(1)} all-reduce(f32[4,8,128]{2,1,0:T(8,128)S(1)} %fusion.70), channel_id=4, replica_groups=mesh['region'=8,'blk'=4] {'blk'}, use_global_device_ids=true, to_apply=%region_15.15.clone | all-reduce | flops 4096 | bytes 32768 | tf_op jit(solution)/shard_map/while
  676.8 6.4 all-reduce.14
  683.1 21.3 %all-reduce.15 = (f32[]{:T(128)}, f32[]{:T(128)}) all-reduce(f32[]{:T(128)} %get-tuple-element.277, f32[]{:T(128)} %get-tuple-element.278), channel_id=1, replica_groups=mesh['region'=8,'blk'=4] {'region'}, use_global_device_ids=true, to_apply=%region_13.13 | all-reduce | flops 2 | bytes 16 | tf_op jit(solution)/shard_map/while/body/eval_jaxpr/psum | solution.py:76
  707.4 5.3 all-gather.4
  721.8 5.4 fusion.68
  735.7 10.1 %all-reduce.13 = f32[4,8,128]{2,1,0:T(8,128)S(1)} all-reduce(f32[4,8,128]{2,1,0:T(8,128)S(1)} %fusion.70), channel_id=4, replica_groups=mesh['region'=8,'blk'=4] {'blk'}, use_global_device_ids=true, to_apply=%region_15.15.clone | all-reduce | flops 4096 | bytes 32768 | tf_op jit(solution)/shard_map/while
  747.0 6.4 all-reduce.14
  753.4 21.3 %all-reduce.15 = (f32[]{:T(128)}, f32[]{:T(128)}) all-reduce(f32[]{:T(128)} %get-tuple-element.277, f32[]{:T(128)} %get-tuple-element.278), channel_id=1, replica_groups=mesh['region'=8,'blk'=4] {'region'}, use_global_device_ids=true, to_apply=%region_13.13 | all-reduce | flops 2 | bytes 16 | tf_op jit(solution)/shard_map/while/body/eval_jaxpr/psum | solution.py:76
  777.7 5.3 all-gather.4
  792.0 5.4 fusion.68
  806.0 10.1 %all-reduce.13 = f32[4,8,128]{2,1,0:T(8,128)S(1)} all-reduce(f32[4,8,128]{2,1,0:T(8,128)S(1)} %fusion.70), channel_id=4, replica_groups=mesh['region'=8,'blk'=4] {'blk'}, use_global_device_ids=true, to_apply=%region_15.15.clone | all-reduce | flops 4096 | bytes 32768 | tf_op jit(solution)/shard_map/while
  817.3 6.4 all-reduce.14
  823.6 21.3 %all-reduce.15 = (f32[]{:T(128)}, f32[]{:T(128)}) all-reduce(f32[]{:T(128)} %get-tuple-element.277, f32[]{:T(128)} %get-tuple-element.278), channel_id=1, replica_groups=mesh['region'=8,'blk'=4] {'region'}, use_global_device_ids=true, to_apply=%region_13.13 | all-reduce | flops 2 | bytes 16 | tf_op jit(solution)/shard_map/while/body/eval_jaxpr/psum | solution.py:76
  847.9 5.3 all-gather.4
  862.3 5.4 fusion.68
  876.2 10.1 %all-reduce.13 = f32[4,8,128]{2,1,0:T(8,128)S(1)} all-reduce(f32[4,8,128]{2,1,0:T(8,128)S(1)} %fusion.70), channel_id=4, replica_groups=mesh['region'=8,'blk'=4] {'blk'}, use_global_device_ids=true, to_apply=%region_15.15.clone | all-reduce | flops 4096 | bytes 32768 | tf_op jit(solution)/shard_map/while
  887.5 6.4 all-reduce.14
  893.9 21.3 %all-reduce.15 = (f32[]{:T(128)}, f32[]{:T(128)}) all-reduce(f32[]{:T(128)} %get-tuple-element.277, f32[]{:T(128)} %get-tuple-element.278), channel_id=1, replica_groups=mesh['region'=8,'blk'=4] {'region'}, use_global_device_ids=true, to_apply=%region_13.13 | all-reduce | flops 2 | bytes 16 | tf_op jit(solution)/shard_map/while/body/eval_jaxpr/psum | solution.py:76
  (328 shorter events, 236.1 us)
Async XLA Ops:
  0.6 52.0 %all-to-all-start = ((f32[32,2,128,128]{3,2,1,0:T(8,128)}), f32[32,2,128,128]{3,2,1,0:T(8,128)}, u32[]{:S(2)}, u32[]{:S(2)}) async-start(f32[32,2,128,128]{3,2,1,0:T(8,128)} %param.7), calls=%async_computation | async-start | bytes 8388608 | tf_op jit(solution)/shard_map/all_to_all | solution.py:49
  55.1 8.2 copy-start.9
  55.1 19.9 %copy-start.4 = (f32[8,128]{1,0:T(8,128)S(1)}, f32[8,128]{1,0:T(8,128)}, u32[]{:S(2)}) copy-start(f32[8,128]{1,0:T(8,128)} %param.10) | copy-start | bytes 12292
  55.1 19.9 %copy-start.7 = (f32[8,128]{1,0:T(8,128)S(1)}, f32[8,128]{1,0:T(8,128)}, u32[]{:S(2)}) copy-start(f32[8,128]{1,0:T(8,128)} %param.11) | copy-start | bytes 12292
  60.2 4.7 collective-permute-start.4
  60.8 4.1 collective-permute-start.5
  80.9 4.4 collective-permute-start.6
  83.8 4.6 collective-permute-start.7
  89.1 5.4 copy-start.1
  97.4 4.7 collective-permute-start.8
  97.5 4.8 collective-permute-start.9
  153.6 4.6 collective-permute-start
  153.7 6.4 collective-permute-start.1
  160.7 5.4 copy-start.2
  169.0 4.7 collective-permute-start.2
  170.2 4.6 collective-permute-start.3
  221.1 6.2 collective-permute-start
  225.8 3.7 collective-permute-start.1
  230.2 5.4 copy-start.2
  238.5 4.5 collective-permute-start.2
  239.5 4.6 collective-permute-start.3
  291.3 6.2 collective-permute-start
  296.0 3.7 collective-permute-start.1
  300.3 5.4 copy-start.2
  308.7 4.5 collective-permute-start.2
  309.6 4.6 collective-permute-start.3
  361.5 6.2 collective-permute-start
  366.2 3.7 collective-permute-start.1
  370.5 5.4 copy-start.2
  378.9 4.5 collective-permute-start.2
  379.8 4.6 collective-permute-start.3
  431.7 6.2 collective-permute-start
  436.4 3.7 collective-permute-start.1
  440.8 5.4 copy-start.2
  449.1 4.5 collective-permute-start.2
  450.1 4.6 collective-permute-start.3
  502.0 6.2 collective-permute-start
  506.7 3.7 collective-permute-start.1
  511.0 5.4 copy-start.2
  519.4 4.5 collective-permute-start.2
  520.3 4.6 collective-permute-start.3
  572.2 6.2 collective-permute-start
  576.9 3.7 collective-permute-start.1
  581.3 5.4 copy-start.2
  589.6 4.5 collective-permute-start.2
  590.6 4.6 collective-permute-start.3
  642.5 6.2 collective-permute-start
  647.2 3.7 collective-permute-start.1
  659.9 4.5 collective-permute-start.2
  660.8 4.6 collective-permute-start.3
  712.7 6.2 collective-permute-start
  717.4 3.7 collective-permute-start.1
  721.8 5.4 copy-start.2
  730.1 4.5 collective-permute-start.2
  731.1 4.6 collective-permute-start.3
  783.0 6.2 collective-permute-start
  787.7 3.7 collective-permute-start.1
  792.0 5.4 copy-start.2
  800.4 4.5 collective-permute-start.2
  801.3 4.6 collective-permute-start.3
  853.2 6.2 collective-permute-start
  857.9 3.7 collective-permute-start.1
  870.6 4.5 collective-permute-start.2
  871.6 4.6 collective-permute-start.3
  (7 other events, 23.7 us)
